TPU v7x, 512 devices: a whole 4x4x16 slice. The times are simulated.
512 devices in a mesh: edp: 32 (over z_hi, y, core), etp: 16 (over z_lo, x).
Axes of the slice: x: 4, y: 4, z: 16 (z_hi: 4, z_lo: 4; z = z_hi * 4 + z_lo), core: 2. Of those that a mesh axis runs over, the one named last changes fastest.
Arguments:
- tokens: bfloat16 [16384, 3072], P('edp'), may hold values from -6 to 6
- expert_ids: int32 [16384, 2], P('edp'), may hold values from 0 to 7, as said below
- route_weight: float32 [16384, 2], P('edp'), may hold values from 0.2 to 1
- index_list: int32 [32, 256], P('edp'), may hold values from 0 to 512, as said below
- gate_weight: bfloat16 [3072, 8192], P('edp', 'etp'), may hold values from -0.109375 to 0.109375
- up_weight: bfloat16 [3072, 8192], P('edp', 'etp'), may hold values from -0.109375 to 0.109375
- down_weight: bfloat16 [8192, 3072], P('etp', 'edp'), may hold values from -0.0625 to 0.0625
Outputs:
- expert_out: bfloat16 [16384, 3072], P(('edp', 'etp'))
Inputs may be any that keep to these rules, and one draw needn't show every extreme that they name: `index_list`: row b lists, increasing, the positions within block b of the tokens that name expert 0, then 512 in the remaining slots; in every draw some block is full. `expert_ids`: each token names two different experts; a token names expert 0 exactly when its position stands in its block's row of index_list.
All inputs are finite; a program needn't handle non-finite values.
Results may differ from a plain program's by a relative error of at most 0.018.
Values may be sent and summed in bfloat16 or wider, within the bound.
No kernel may reach another device: no remote copies, remote signals or barrier semaphores. Data moves between devices by JAX's collectives and lax.ppermute only.
A program may use at most 64 MiB of HBM per device.

v0:
```python
import jax
import jax.numpy as jnp
from jax import lax
from jax.sharding import PartitionSpec as P


def gather_turned(arrays, axis, dims):
    turned = [jnp.moveaxis(a, dim, 0) for a, dim in zip(arrays, dims)]
    widths = [t[0].size for t in turned]
    both = jnp.concatenate([t.reshape(-1, w) for t, w in zip(turned, widths)], axis=1)
    result = lax.all_gather(both, axis, axis=0, tiled=True)
    blocks = jnp.split(result, [sum(widths[:k]) for k in range(1, len(widths))], axis=1)
    return tuple(
        (
            jnp.moveaxis(b.reshape(-1, *t.shape[1:]), 0, dim)
            for b, t, dim in zip(blocks, turned, dims)
        )
    )


def in_blocks(value, dim, devices):
    before, after = (value.shape[:dim], value.shape[dim + 1 :])
    return jnp.moveaxis(value.reshape(*before, devices, -1, *after), dim, 0)


def sum_at_owner(value, axis, dim):
    devices = lax.axis_size(axis)
    blocks = lax.all_to_all(in_blocks(value, dim, devices), axis, 0, 0, tiled=True)
    return jnp.sum(blocks.astype(jnp.float32), axis=0)


def shards(tokens, expert_ids, route_weight, index_list, gate_weight, up_weight, down_weight):
    block_rows = tokens.shape[0]
    slot_rows = index_list[0]
    combine = jnp.sum(
        jnp.where(expert_ids == 0, route_weight, jnp.zeros_like(route_weight)), axis=1
    )
    is_live = slot_rows < block_rows
    safe_rows = jnp.minimum(slot_rows, block_rows - 1)
    inputs = jnp.take(tokens, safe_rows, axis=0)
    row_scale = jnp.where(is_live, jnp.take(combine, safe_rows), jnp.zeros_like(combine[:1]))
    gate_full, up_full, down_full = gather_turned(
        (gate_weight, up_weight, down_weight), "edp", (0, 0, 1)
    )
    gate_sum = jnp.dot(inputs, gate_full, preferred_element_type=jnp.float32)
    up_sum = jnp.dot(inputs, up_full, preferred_element_type=jnp.float32)
    hidden = (jax.nn.silu(gate_sum) * up_sum * row_scale[:, None]).astype(jnp.bfloat16)
    partial_terms = jnp.dot(hidden, down_full, preferred_element_type=jnp.float32)
    placing = (jnp.arange(block_rows)[:, None] == slot_rows[None, :]).astype(jnp.float32)
    partial_terms = jnp.dot(placing, partial_terms, preferred_element_type=jnp.float32)
    shares = sum_at_owner(partial_terms.astype(jnp.bfloat16), "etp", 0)
    return shares.astype(jnp.bfloat16)


def solution(mesh):
    in_specs = (
        P("edp", None),
        P("edp", None),
        P("edp", None),
        P("edp", None),
        P("edp", "etp"),
        P("edp", "etp"),
        P("etp", "edp"),
    )
    out_specs = P(("edp", "etp"), None)
    return jax.shard_map(shards, mesh=mesh, in_specs=in_specs, out_specs=out_specs, check_vma=False)
```

profile of v0, /device:TPU:16, one launch (start us, length us, event | category | flops | bytes accessed | tf_op | source)
XLA Modules:
  0.0 259.0 jit_solution(4967588532074355939)
XLA Ops:
  6.5 0.0 copy-start
  6.5 0.0 all-gather.2.cloned.1.call-start
  6.5 1.9 pad_maximum_fusion
  8.4 0.0 all-gather.2.cloned.1.call-update
  8.4 0.7 compare_select_fusion.1
  9.1 0.7 fusion.18
  9.9 1.9 gather_fusion.1
  11.8 0.0 copy-done
  11.8 0.0 copy-start.2
  11.8 2.7 %gather_fusion = bf16[256,3072]{1,0:T(8,128)(2,1)} fusion(bf16[512,3072]{1,0:T(8,128)(2,1)S(1)} %copy-done, s32[1024]{0:T(1024)S(1)} %pad_clamp_fusion), kind=kCustom, calls=%fused_computation | custom fusion | bytes 3146752 | tf_op jit(solution)/shard_map/jit(_take)/gather | solution.py:40
  14.6 0.0 copy-done.2
  14.6 146.0 %all-gather.2.cloned.1.call-done = bf16[3072,1536]{1,0:T(8,128)(2,1)} async-done(((bf16[96,1536]{1,0:T(8,128)(2,1)}), bf16[3072,1536]{1,0:T(8,128)(2,1)}) %all-gather.2.cloned.1.call-update) | async-done | bytes 9437200 | tf_op jit(solution)/shard_map/all_gather | solution.py:11
  160.6 0.0 copy-start.1
  160.6 3.5 %fusion.4 = f32[256,512]{1,0:T(8,128)S(1)} fusion(bf16[3072,1536]{1,0:T(8,128)(2,1)} %all-gather.2.cloned.1.call-done, bf16[256,3072]{1,0:T(8,128)(2,1)} %gather_fusion, pred[256]{0:T(512)(128)(4,1)S(1)} %compare_and_fusion), kind=kOutput, calls=%fused_computation.7 | convolution fusion | flops 806092800 | bytes 5243136 | tf_op jit(solution)/shard_map/dot_general | solution.py:45
  164.1 0.0 copy-done.1
  164.1 2.9 %fusion.14 = bf16[256,512]{1,0:T(8,128)(2,1)S(1)} fusion(bf16[3072,1536]{1,0:T(8,128)(2,1)} %all-gather.2.cloned.1.call-done, bf16[256,3072]{1,0:T(8,128)(2,1)S(1)} %copy-done.1, pred[256]{0:T(512)(128)(4,1)S(1)} %compare_and_fusion, f32[256,512]{1,0:T(8,128)S(1)} %fusion.4, f32[256]{0:T(256)S(1)} %compare_select_fusion.3), kind=kOutput, calls=%fused_computation.12 | convolution fusion | flops 807010304 | bytes 5506304 | tf_op jit(solution)/shard_map/dot_general | solution.py:46
  167.0 5.4 %convolution_convert_fusion = bf16[512,3072]{1,0:T(8,128)(2,1)} fusion(bf16[256,512]{1,0:T(8,128)(2,1)S(1)} %fusion.14, bf16[3072,1536]{1,0:T(8,128)(2,1)} %all-gather.2.cloned.1.call-done, s32[256]{0:T(256)S(1)} %bitcast.11), kind=kOutput, calls=%fused_computation.2 | convolution fusion | flops 1612316672 | bytes 6554624 | tf_op jit(solution)/shard_map/dot_general | solution.py:50
  172.4 76.6 %all_to_all.5 = bf16[16,32,3072]{2,1,0:T(8,128)(2,1)} all-to-all(bf16[16,32,3072]{2,1,0:T(8,128)(2,1)} %bitcast.7), channel_id=1, replica_groups=mesh['edp'=32,'etp'=16] {'etp'}, dimensions={0} | all-to-all | bytes 6291456 | tf_op jit(solution)/shard_map/all_to_all | solution.py:28
  249.0 3.2 %reduce_sum.22 = bf16[32,3072]{1,0:T(8,128)(2,1)} reduce(bf16[16,32,3072]{2,1,0:T(8,128)(2,1)} %all_to_all.5, bf16[]{:T(256)} %constant.41.clone.1), dimensions={0}, to_apply=%region_1.2 | reduce | flops 1474560 | bytes 3342338 | tf_op jit(solution)/shard_map/reduce_sum | solution.py:29
  (3 shorter events, 0.0 us)
Async XLA Ops:
  6.5 5.3 %copy-start = (bf16[512,3072]{1,0:T(8,128)(2,1)S(1)}, bf16[512,3072]{1,0:T(8,128)(2,1)}, u32[]{:S(2)}) copy-start(bf16[512,3072]{1,0:T(8,128)(2,1)} %param.7) | copy-start | bytes 9437188
  6.5 154.0 %all-gather.2.cloned.1.call-start = ((), (), s32[]{:S(2)}) async-start(), calls=%async_computation.1 | async-start | bytes 9732096 | tf_op jit(solution)/shard_map/all_gather | solution.py:11
  11.8 2.8 %copy-start.2 = (s32[1,256]{1,0:T(1,128)S(1)}, s32[1,256]{1,0:T(1,128)}, u32[]{:S(2)}) copy-start(s32[1,256]{1,0:T(1,128)} %param.10) | copy-start | bytes 3076
  160.6 3.5 %copy-start.1 = (bf16[256,3072]{1,0:T(8,128)(2,1)S(1)}, bf16[256,3072]{1,0:T(8,128)(2,1)}, u32[]{:S(2)}) copy-start(bf16[256,3072]{1,0:T(8,128)(2,1)} %gather_fusion) | copy-start | bytes 4718596
Sparse Core Ops, SparseCore 0:
  10.5 150.0 all-gather.1
where the time goes:
time: 259 us
  waiting for transfers between devices  146 us (56%)
  blocking collectives  76.6 us (30%)
  between operations  13.5 us (5%)
  matrix products  11.8 us (5%)
  other arithmetic  6.5 us (3%)
  local copies, waits for them, and re-layouts  4.7 us (2%)
    all_gather x1, waiting for transfers between devices, gather_turned(): result = lax.all_gather(both, axis, axis=0, tiled=True)  146 us
    all_to_all x1, blocking collectives, sum_at_owner(): lax.all_to_all(in_blocks(value, dim, devices), axis, 0, 0, tiled=True)  76.6 us
    dot_general x1, matrix products, shards(): jnp.dot(placing, partial_terms, preferred_element_type=jnp.float32)  5.36 us
  transfers between devices with their start and end apart: 1, of which 1 were waited for; matrix products, arithmetic and copies ran while one was open for 2% of the time, Pallas kernels for 0%

commit v1 on v0

--- a/solution.py
+++ b/solution.py
@@ -8,7 +8,8 @@
     turned = [jnp.moveaxis(a, dim, 0) for a, dim in zip(arrays, dims)]
     widths = [t[0].size for t in turned]
     both = jnp.concatenate([t.reshape(-1, w) for t, w in zip(turned, widths)], axis=1)
-    result = lax.all_gather(both, axis, axis=0, tiled=True)
+    near = jnp.stack([both for _ in range(jax.lax.axis_size(axis))], axis=0)
+    result = jnp.concatenate(jax.lax.all_to_all(near, axis, 0, 0), axis=0)
     blocks = jnp.split(result, [sum(widths[:k]) for k in range(1, len(widths))], axis=1)
     return tuple(
         (

time: 259 us -> 532 us (2.05)
  the two profiles are of different devices: /device:TPU:16 before, /device:TPU:1 now
where the time goes in v1:
time: 532 us
  waiting for transfers between devices  409 us (77%)
  blocking collectives  77.8 us (15%)
  starting transfers between devices  19.5 us (4%)
  matrix products  11.8 us (2%)
  local copies, waits for them, and re-layouts  9.39 us (2%)
    all_to_all x1, waiting for transfers between devices, gather_turned(): result = jnp.concatenate(jax.lax.all_to_all(near, axis, 0, 0), axis=0)  409 us
    all_to_all x1, blocking collectives, sum_at_owner(): lax.all_to_all(in_blocks(value, dim, devices), axis, 0, 0, tiled=True)  77.8 us
    all_to_all x1, starting transfers between devices, gather_turned(): result = jnp.concatenate(jax.lax.all_to_all(near, axis, 0, 0), axis=0)  19.5 us
  transfers between devices with their start and end apart: 1, of which 1 were waited for; matrix products, arithmetic and copies ran while one was open for 1% of the time, Pallas kernels for 0%

profile of v1, /device:TPU:1, one launch (start us, length us, event | category | flops | bytes accessed | tf_op | source)
XLA Modules:
  0.0 531.6 jit_solution(3503778399082322326)
XLA Ops:
  0.0 0.0 copy-start
  0.0 1.2 pad_maximum_fusion
  1.2 4.7 stack.2
  5.9 0.0 copy-start.2
  5.9 19.5 %all-to-all-start = ((bf16[32,96,1536]{2,1,0:T(8,128)(2,1)}), bf16[32,96,1536]{2,1,0:T(8,128)(2,1)}, u32[]{:S(2)}, u32[]{:S(2)}) async-start(bf16[32,96,1536]{2,1,0:T(8,128)(2,1)} %stack.2), calls=%async_computation | async-start | bytes 18874368 | tf_op jit(solution)/shard_map/all_to_all | solution.py:12
  25.4 0.0 copy-done.2
  25.5 0.0 copy-done
  25.5 0.0 copy-start.3
  25.5 0.0 copy-start.4
  25.5 2.7 gather_fusion
  28.2 0.0 copy-done.3
  28.2 0.0 copy-done.4
  28.2 1.9 gather_fusion.1
  30.2 408.6 %all-to-all-done = bf16[32,96,1536]{2,1,0:T(8,128)(2,1)} async-done(((bf16[32,96,1536]{2,1,0:T(8,128)(2,1)}), bf16[32,96,1536]{2,1,0:T(8,128)(2,1)}, u32[]{:S(2)}, u32[]{:S(2)}) %all-to-all-start) | async-done | bytes 9437216 | tf_op jit(solution)/shard_map/all_to_all | solution.py:12
  438.8 0.0 copy-start.1
  438.8 3.5 fusion.4
  442.3 0.0 copy-done.1
  442.3 2.9 fusion.14
  445.2 5.4 %convolution_convert_fusion = bf16[512,3072]{1,0:T(8,128)(2,1)} fusion(bf16[256,512]{1,0:T(8,128)(2,1)S(1)} %fusion.14, bf16[3072,1536]{1,0:T(8,128)(2,1)} %bitcast.4, s32[256]{0:T(256)S(1)} %bitcast.12), kind=kOutput, calls=%fused_computation.2 | convolution fusion | flops 1612316672 | bytes 6554624 | tf_op jit(solution)/shard_map/dot_general | solution.py:51
  450.6 77.8 %all_to_all.10 = bf16[16,32,3072]{2,1,0:T(8,128)(2,1)} all-to-all(bf16[16,32,3072]{2,1,0:T(8,128)(2,1)} %bitcast.8), channel_id=1, replica_groups=mesh['edp'=32,'etp'=16] {'etp'}, dimensions={0} | all-to-all | bytes 6291456 | tf_op jit(solution)/shard_map/all_to_all | solution.py:29
  528.4 3.2 reduce_sum.22
  (5 shorter events, 0.0 us)
Async XLA Ops:
  0.0 25.5 %copy-start = (bf16[512,3072]{1,0:T(8,128)(2,1)S(1)}, bf16[512,3072]{1,0:T(8,128)(2,1)}, u32[]{:S(2)}) copy-start(bf16[512,3072]{1,0:T(8,128)(2,1)} %param.7) | copy-start | bytes 9437188
  5.9 19.6 %copy-start.2 = (s32[1,256]{1,0:T(1,128)S(1)}, s32[1,256]{1,0:T(1,128)}, u32[]{:S(2)}) copy-start(s32[1,256]{1,0:T(1,128)} %param.10) | copy-start | bytes 3076
  5.9 432.9 %all-to-all-start = ((bf16[32,96,1536]{2,1,0:T(8,128)(2,1)}), bf16[32,96,1536]{2,1,0:T(8,128)(2,1)}, u32[]{:S(2)}, u32[]{:S(2)}) async-start(bf16[32,96,1536]{2,1,0:T(8,128)(2,1)} %stack.2), calls=%async_computation | async-start | bytes 18874368 | tf_op jit(solution)/shard_map/all_to_all | solution.py:12
  25.5 2.7 copy-start.3
  25.5 2.7 copy-start.4
  438.8 3.5 copy-start.1
